TPU v7x, 128 devices: a whole 4x4x4 slice. The times are simulated.
128 devices in a mesh: group: 16 (over x, z_lo, core), head: 8 (over y, z_hi).
Axes of the slice: x: 4, y: 4, z: 4 (z_hi: 2, z_lo: 2; z = z_hi * 2 + z_lo), core: 2. Of those that a mesh axis runs over, the one named last changes fastest.
Arguments:
- hidden_in: bfloat16 [256, 2560], P('group'), may hold values from -6 to 6
- ssm_state: float32 [256, 80, 64, 128], P('group', 'head'), may hold values from -6 to 6
- conv_x_state: bfloat16 [256, 3, 5120], P('group', None, 'head'), may hold values from -6 to 6
- conv_bc_state: bfloat16 [256, 3, 256], P('group'), may hold values from -6 to 6
- token_ids: int32 [256], P('group'), may hold values from 0 to 25599
- ref_logits: bfloat16 [256, 25600], P('group', 'head'), may hold values from -15 to 350
- in_z: bfloat16 [2560, 5120], P('group', 'head'), may hold values from -0.125 to 0.125
- in_x: bfloat16 [2560, 5120], P('group', 'head'), may hold values from -0.125 to 0.125
- in_bc: bfloat16 [2560, 256], P('group'), may hold values from -0.125 to 0.125
- in_dt: bfloat16 [2560, 80], P('group', 'head'), may hold values from -0.125 to 0.125
- out_t: bfloat16 [2560, 5120], P('group', 'head'), may hold values from -0.078125 to 0.078125
- lm_head: bfloat16 [25600, 2560], P('head', 'group'), may hold values from -6 to 6
- conv_wx: float32 [4, 5120], P(None, 'head'), may hold values from -3 to 3
- conv_bx: float32 [5120], P('head'), may hold values from -1.5 to 1.5
- conv_wbc: float32 [4, 256], replicated, may hold values from -3 to 3
- conv_bbc: float32 [256], replicated, may hold values from -1.5 to 1.5
- dt_bias: float32 [80], P('head'), may hold values from -4 to -1
- a_log: float32 [80], P('head'), may hold values from 0 to 2.77
- skip_gain: float32 [80], P('head'), may hold values from 0.5 to 1.5
- norm_in: float32 [2560], replicated, may hold values from 0.5 to 1.5
- norm_gain: float32 [5120], P('head'), may hold values from 0.5 to 1.5
- final_gain: float32 [2560], replicated, may hold values from 0.5 to 1.5
Outputs:
- new_state: float32 [256, 80, 64, 128], P('group', 'head')
- divergence: float32 [256], P('group')
- token_logprob: float32 [256], P('group')
- roll_z: bfloat16 [2560, 5120], P(None, 'head')
- roll_x: bfloat16 [2560, 5120], P(None, 'head')
- roll_bc: bfloat16 [2560, 256], replicated
- roll_dt: bfloat16 [2560, 80], P(None, 'head')
- roll_out: bfloat16 [2560, 5120], P(None, 'head')
All inputs are finite; a program needn't handle non-finite values.
Results may differ from a plain program's by a relative error of at most 0.0102.
Values may be sent and summed in bfloat16 or wider, within the bound.
A program may use at most 128 MiB of HBM per device.

v0:
```python
import jax
import jax.numpy as jnp
from jax import lax
from jax.sharding import PartitionSpec as P

P_SIZE = 64
EPSILON = 1e-05


def sent_together(arrays, axis, dim, along):
    both = jnp.concatenate(arrays, axis=along)
    result, at, done = (lax.all_gather(both, axis, axis=dim, tiled=True), 0, [])
    for a in arrays:
        done.append(lax.slice_in_dim(result, at, at + a.shape[along], axis=along))
        at += a.shape[along]
    return tuple(done)


def from_everyone(array, axis):
    peers = lax.axis_size(axis)
    return lax.all_to_all(
        jnp.broadcast_to(array[None], (peers, *array.shape)), axis, 0, 0, tiled=True
    )


def taken_together(array, axis):
    everything = from_everyone(array, axis)
    return jnp.sum(everything, axis=0)


def collected_together(array, axis):
    leaves = jax.tree.leaves(array)
    sequence = sorted(range(len(leaves)), key=lambda k: -leaves[k].size)
    width = (1, *leaves[sequence[0]].shape)[-1]
    lines = [
        jnp.pad(leaves[k].reshape(-1), (0, -leaves[k].size % width)).reshape(-1, width)
        for k in sequence
    ]
    both, at, found = (from_everyone(jnp.concatenate(lines), axis), 0, {})
    for k, line in zip(sequence, lines):
        piece = both[:, at : at + len(line)].reshape(len(both), -1)
        found[k] = piece[:, : leaves[k].size].reshape(-1, *leaves[k].shape)
        at += len(line)
    numbers = iter(range(len(leaves)))
    return jax.tree.map(lambda _: found[next(numbers)], array)


def folded_in_pairs(pieces, combine):
    while len(jax.tree.leaves(pieces)[0]) > 1:
        pieces = jax.vmap(combine)(
            *(jax.tree.map(lambda part: part[side::2], pieces) for side in (0, 1))
        )
    return jax.tree.map(lambda part: part[0], pieces)


def combined_all(array, axis, combine):
    pieces = collected_together(array, axis)
    return folded_in_pairs(pieces, combine)


def rms_norm(values, gain):
    return values * lax.rsqrt(jnp.mean(values * values, axis=-1, keepdims=True) + EPSILON) * gain


def causal_conv(history, newest, taps, offset):
    window = jnp.concatenate([history, newest[:, None, :]], axis=1).astype(jnp.float32)
    return jax.nn.silu(jnp.sum(window * taps[None, :, :], axis=1) + offset)


def combine_stats(first, second):
    roll_max = jnp.maximum(first[0], second[0])
    roll_sum = first[1] * jnp.exp(first[0] - roll_max) + second[1] * jnp.exp(second[0] - roll_max)
    ref_max = jnp.maximum(first[2], second[2])
    scale_first = jnp.exp(first[2] - ref_max)
    scale_second = jnp.exp(second[2] - ref_max)
    ref_sum = first[3] * scale_first + second[3] * scale_second
    cross_sum = first[4] * scale_first + second[4] * scale_second
    return (roll_max, roll_sum, ref_max, ref_sum, cross_sum, first[5] + second[5])


def shards(
    hidden_in,
    ssm_state,
    conv_x_state,
    conv_bc_state,
    token_ids,
    ref_logits,
    in_z,
    in_x,
    in_bc,
    in_dt,
    out_t,
    lm_head,
    conv_wx,
    conv_bx,
    conv_wbc,
    conv_bbc,
    dt_bias,
    a_log,
    skip_gain,
    norm_in,
    norm_gain,
    final_gain,
):
    roll_z, roll_x, roll_bc, roll_dt, roll_out = sent_together(
        (in_z, in_x, in_bc, in_dt, out_t), "group", 0, 1
    )
    stream_in = hidden_in.astype(jnp.float32)
    normed = rms_norm(stream_in, norm_in).astype(jnp.bfloat16)
    gate_branch = jnp.dot(normed, roll_z, preferred_element_type=jnp.float32).astype(jnp.bfloat16)
    x_branch = jnp.dot(normed, roll_x, preferred_element_type=jnp.float32).astype(jnp.bfloat16)
    bc_branch = jnp.dot(normed, roll_bc, preferred_element_type=jnp.float32).astype(jnp.bfloat16)
    step_raw = jnp.dot(normed, roll_dt, preferred_element_type=jnp.float32).astype(jnp.bfloat16)
    x_conv = causal_conv(conv_x_state, x_branch, conv_wx, conv_bx)
    bc_conv = causal_conv(conv_bc_state, bc_branch, conv_wbc, conv_bbc)
    state_size = bc_conv.shape[1] // 2
    b_vals = bc_conv[:, :state_size]
    c_vals = bc_conv[:, state_size:]
    step = jax.nn.softplus(step_raw.astype(jnp.float32) + dt_bias)
    decay = jnp.exp(-step * jnp.exp(a_log))
    seq_count = x_conv.shape[0]
    local_heads = a_log.shape[0]
    x_heads = x_conv.reshape(seq_count, local_heads, P_SIZE)
    inflow = (step[:, :, None] * x_heads)[:, :, :, None] * b_vals[:, None, None, :]
    new_state = decay[:, :, None, None] * ssm_state + inflow
    ssm_out = jnp.einsum("shpn,sn->shp", new_state, c_vals)
    ssm_out = (ssm_out + skip_gain[None, :, None] * x_heads).reshape(
        seq_count, local_heads * P_SIZE
    )
    gated = ssm_out * jax.nn.silu(gate_branch.astype(jnp.float32))
    square_total = taken_together(jnp.sum(gated * gated, axis=-1), "head")
    inner_width = gated.shape[1] * lax.axis_size("head")
    gated_out = (
        gated * lax.rsqrt(square_total / inner_width + EPSILON)[:, None] * norm_gain
    ).astype(jnp.bfloat16)
    partial_mix = lax.dot_general(
        gated_out, roll_out, (((1,), (1,)), ((), ())), preferred_element_type=jnp.float32
    )
    mixed = taken_together(partial_mix, "head")
    final_hidden = rms_norm(stream_in + mixed, final_gain).astype(jnp.bfloat16)
    vocab_local = lm_head.shape[0]
    logits = lax.dot_general(
        final_hidden,
        lax.all_gather(lm_head, "group", axis=1, tiled=True),
        (((1,), (1,)), ((), ())),
        preferred_element_type=jnp.float32,
    )
    reference_rows = ref_logits.astype(jnp.float32)
    column_ids = lax.axis_index("head") * vocab_local + lax.broadcasted_iota(
        jnp.int32, (1, vocab_local), 1
    )
    picked_part = jnp.sum(jnp.where(column_ids == token_ids[:, None], logits, 0.0), axis=-1)
    roll_local = jnp.max(logits, axis=-1)
    ref_local = jnp.max(reference_rows, axis=-1)
    roll_sum = jnp.sum(jnp.exp(logits - roll_local[:, None]), axis=-1)
    ref_weights = jnp.exp(reference_rows - ref_local[:, None])
    ref_sum = jnp.sum(ref_weights, axis=-1)
    cross_sum = jnp.sum(ref_weights * (reference_rows - logits), axis=-1)
    roll_max, roll_sum, ref_max, ref_sum, cross_sum, picked = combined_all(
        (roll_local, roll_sum, ref_local, ref_sum, cross_sum, picked_part), "head", combine_stats
    )
    lse_roll = roll_max + jnp.log(roll_sum)
    lse_ref = ref_max + jnp.log(ref_sum)
    divergence = cross_sum / ref_sum - lse_ref + lse_roll
    token_logprob = picked - lse_roll
    return (new_state, divergence, token_logprob, roll_z, roll_x, roll_bc, roll_dt, roll_out)


def solution(mesh):
    return jax.shard_map(
        shards,
        mesh=mesh,
        in_specs=(
            P("group", None),
            P("group", "head", None, None),
            P("group", None, "head"),
            P("group", None, None),
            P("group"),
            P("group", "head"),
            P("group", "head"),
            P("group", "head"),
            P("group", None),
            P("group", "head"),
            P("group", "head"),
            P("head", "group"),
            P(None, "head"),
            P("head"),
            P(),
            P(),
            P("head"),
            P("head"),
            P("head"),
            P(),
            P("head"),
            P(),
        ),
        out_specs=(
            P("group", "head", None, None),
            P("group"),
            P("group"),
            P(None, "head"),
            P(None, "head"),
            P(),
            P(None, "head"),
            P(None, "head"),
        ),
        check_vma=False,
    )
```

profile of v0, /device:TPU:0, one launch (start us, length us, event | category | flops | bytes accessed | tf_op | source)
XLA Modules:
  0.0 219.2 jit_solution(8908940668585763981)
XLA Ops:
  7.2 0.8 copy.50
  8.1 2.1 concatenate.12
  10.2 0.7 all-gather.5.cloned.1.call-update
  10.9 0.5 exp.69
  11.7 69.3 %all-gather.3.cloned.1.call-done = bf16[2560,2186]{1,0:T(8,128)(2,1)} async-done(((bf16[160,2186]{1,0:T(8,128)(2,1)}), bf16[2560,2186]{1,0:T(8,128)(2,1)}) %all-gather.3.cloned.1.call-update) | async-done | bytes 11192336 | tf_op jit(solution)/shard_map/all_gather | solution.py:12
  81.0 6.3 %fusion.26 = (bf16[2560,640]{1,0:T(8,128)(2,1)S(1)}, bf16[2560,640]{1,0:T(8,128)(2,1)}, bf16[2560,640]{1,0:T(8,128)(2,1)S(1)}) fusion(bf16[2560,2186]{1,0:T(8,128)(2,1)} %all-gather.3.cloned.1.call-done), kind=kLoop, calls=%fused_computation.67 | loop fusion | bytes 19660800 | tf_op jit(solution)/shard_map/slice | solution.py:14
  87.3 1.7 copy-done.2
  89.0 0.6 fusion.1
  89.7 1.4 slice.210
  91.1 0.3 fusion.2
  91.5 0.7 divide_multiply_fusion.1
  92.2 1.6 multiply_exponential_fusion
  93.9 4.2 %multiply_add_fusion = f32[16,10,64,128]{3,2,1,0:T(8,128)S(1)} fusion(f32[16,10,64,128]{3,2,1,0:T(8,128)} %param.23, f32[16,128]{1,0:T(8,128)S(1)} %get-tuple-element.72, f32[16,10,64]{2,1,0:T(8,128)S(1)} %broadcast_multiply_fusion, f32[16,10]{1,0:T(8,128)S(1)} %get-tuple-element.75), kind=kLoop, calls=%fused_computation | loop fusion | flops 3932160 | bytes 10535552 | tf_op jit(solution)/shard_map/add | solution.py:125
  98.1 2.3 %copy-done = f32[16,10,64,128]{3,2,1,0:T(8,128)} copy-done((f32[16,10,64,128]{3,2,1,0:T(8,128)}, f32[16,10,64,128]{3,2,1,0:T(8,128)S(1)}, u32[]{:S(2)}) %copy-start) | copy-done | bytes 5242904
  100.5 2.1 fusion.30
  102.6 0.7 bitcast_add_fusion
  103.3 1.0 reshape.143
  104.3 0.7 multiply_reduce_fusion.3
  105.0 14.1 %all_to_all.16 = f32[8,1,16]{2,1,0:T(1,128)S(1)} all-to-all(f32[8,1,16]{2,1,0:T(1,128)S(1)} %broadcast_in_dim.15), channel_id=1, replica_groups=mesh['group'=16,'head'=8] {'head'}, dimensions={0} | all-to-all | bytes 1024 | tf_op jit(solution)/shard_map/all_to_all | solution.py:21
  119.2 3.0 %fusion.15 = f32[16,2560]{1,0:T(8,128)S(1)} fusion(bf16[2560,640]{1,0:T(8,128)(2,1)} %get-tuple-element.63, f32[16,640]{1,0:T(8,128)S(1)} %get-tuple-element.78, f32[640]{0:T(1024)S(1)} %copy-done.11, f32[16]{0:T(128)S(1)} %add_rsqrt_fusion.1), kind=kOutput, calls=%fused_computation.38 | convolution fusion | flops 52459520 | bytes 3484224 | tf_op jit(solution)/shard_map/dot_general | solution.py:136
  122.2 1.2 broadcast_in_dim.16
  123.5 3.6 %all-to-all-start.1 = ((f32[8,16,2560]{2,1,0:T(8,128)}), f32[8,16,2560]{2,1,0:T(8,128)S(1)}, u32[]{:S(2)}, u32[]{:S(2)}) async-start(f32[8,16,2560]{2,1,0:T(8,128)} %broadcast_in_dim.16), calls=%async_computation.1 | async-start | bytes 2621440 | tf_op jit(solution)/shard_map/all_to_all | solution.py:21
  127.2 21.8 %all-to-all-done.1 = f32[8,16,2560]{2,1,0:T(8,128)S(1)} async-done(((f32[8,16,2560]{2,1,0:T(8,128)}), f32[8,16,2560]{2,1,0:T(8,128)S(1)}, u32[]{:S(2)}, u32[]{:S(2)}) %all-to-all-start.1) | async-done | bytes 1310752 | tf_op jit(solution)/shard_map/all_to_all | solution.py:21
  149.3 38.0 %all-gather.5.cloned.1.call-done = bf16[3200,2560]{0,1:T(8,128)(2,1)} async-done(((bf16[3200,160]{0,1:T(8,128)(2,1)}), bf16[3200,2560]{0,1:T(8,128)(2,1)}) %all-gather.5.cloned.1.call-update) | async-done | bytes 16384016 | tf_op jit(solution)/shard_map/all_gather | solution.py:144
  187.3 8.0 %fusion.29 = (f32[16]{0:T(128)S(1)}, f32[16,3200]{1,0:T(8,128)S(1)}) fusion(bf16[3200,2560]{0,1:T(8,128)(2,1)} %all-gather.5.cloned.1.call-done, f32[16,2560]{1,0:T(8,128)S(1)} %reduce_sum.107, bf16[16,2560]{1,0:T(8,128)(2,1)S(1)} %copy-done.4, f32[2560]{0:T(1024)S(1)} %copy-done.8, f32[16]{0:T(128)S(1)} %add_rsqrt_fusion), kind=kOutput, calls=%fused_computation.70 | convolution fusion | flops 262399984 | bytes 16844928 | tf_op jit(solution)/shard_map/dot_general | solution.py:142
  195.4 0.3 select_reduce_fusion
  195.7 0.6 broadcast_in_dim.18
  196.3 6.6 %all-to-all-start.2 = ((f32[8,6,16]{2,1,0:T(8,128)}), f32[8,6,16]{2,1,0:T(8,128)S(1)}, u32[]{:S(2)}, u32[]{:S(2)}) async-start(f32[8,6,16]{2,1,0:T(8,128)} %broadcast_in_dim.18), calls=%async_computation.2 | async-start | bytes 65536 | tf_op jit(solution)/shard_map/all_to_all | solution.py:21
  202.9 0.9 copy.58
  203.8 6.8 %all-to-all-done.2 = f32[8,6,16]{2,1,0:T(8,128)S(1)} async-done(((f32[8,6,16]{2,1,0:T(8,128)}), f32[8,6,16]{2,1,0:T(8,128)S(1)}, u32[]{:S(2)}, u32[]{:S(2)}) %all-to-all-start.2) | async-done | bytes 3104 | tf_op jit(solution)/shard_map/all_to_all | solution.py:21
  211.3 0.5 subtract_bitcast_fusion
  211.9 0.5 add_bitcast_fusion
  (88 shorter events, 1.7 us)
Async XLA Ops:
  7.2 3.7 %copy-start.16 = (f32[10]{0:T(128)S(1)}, f32[10]{0:T(128)}, u32[]{:S(2)}) copy-start(f32[10]{0:T(128)} %param.39) | copy-start | bytes 124
  7.2 4.3 %copy-start.12 = (f32[640]{0:T(1024)S(1)}, f32[640]{0:T(1024)}, u32[]{:S(2)}) copy-start(f32[640]{0:T(1024)} %param.35) | copy-start | bytes 7684
  7.2 4.3 %copy-start.4 = (bf16[16,2560]{1,0:T(8,128)(2,1)S(1)}, bf16[16,2560]{1,0:T(8,128)(2,1)}, u32[]{:S(2)}) copy-start(bf16[16,2560]{1,0:T(8,128)(2,1)} %param.22) | copy-start | bytes 245764
  7.2 73.8 %all-gather.3.cloned.1.call-start = ((), (), s32[]{:S(2)}) async-start(), calls=%async_computation.3 | async-start | bytes 12533760 | tf_op jit(solution)/shard_map/all_gather | solution.py:12
  10.2 177.2 %all-gather.5.cloned.1.call-start = ((), (), s32[]{:S(2)}) async-start(), calls=%async_computation.4 | async-start | bytes 17408000 | tf_op jit(solution)/shard_map/all_gather | solution.py:144
  11.7 77.3 %copy-start.6 = (f32[2560]{0:T(1024)S(1)}, f32[2560]{0:T(1024)}, u32[]{:S(2)}) copy-start(f32[2560]{0:T(1024)} %param.41) | copy-start | bytes 30724
  87.3 1.7 copy-start.2
  87.3 17.1 %copy-start.1 = (bf16[2560,640]{1,0:T(8,128)(2,1)}, bf16[2560,640]{1,0:T(8,128)(2,1)S(1)}, u32[]{:S(2)}) copy-start(bf16[2560,640]{1,0:T(8,128)(2,1)S(1)} %get-tuple-element.62) | copy-start | bytes 9830404
  87.3 2.3 %copy-start.7 = (bf16[16,3,640]{2,0,1:T(8,128)(2,1)S(1)}, bf16[16,3,640]{2,0,1:T(8,128)(2,1)}, u32[]{:S(2)}) copy-start(bf16[16,3,640]{2,0,1:T(8,128)(2,1)} %param.24) | copy-start | bytes 184324
  87.3 2.3 %copy-start.10 = (f32[4,640]{1,0:T(4,128)S(1)}, f32[4,640]{1,0:T(4,128)}, u32[]{:S(2)}) copy-start(f32[4,640]{1,0:T(4,128)} %param.34) | copy-start | bytes 30724
  89.7 1.8 copy-start.9
  89.7 1.8 copy-start.13
  91.1 7.0 %copy-start.3 = (bf16[2560,256]{1,0:T(8,128)(2,1)}, bf16[2560,256]{1,0:T(8,128)(2,1)S(1)}, u32[]{:S(2)}) copy-start(bf16[2560,256]{1,0:T(8,128)(2,1)S(1)} %slice.210) | copy-start | bytes 3932164
  98.1 2.4 %copy-start = (f32[16,10,64,128]{3,2,1,0:T(8,128)}, f32[16,10,64,128]{3,2,1,0:T(8,128)S(1)}, u32[]{:S(2)}) copy-start(f32[16,10,64,128]{3,2,1,0:T(8,128)S(1)} %multiply_add_fusion) | copy-start | bytes 15728644
  98.1 4.5 %copy-start.14 = (f32[10]{0:T(128)S(1)}, f32[10]{0:T(128)}, u32[]{:S(2)}) copy-start(f32[10]{0:T(128)} %param.40) | copy-start | bytes 124
  102.6 16.6 %copy-start.11 = (f32[640]{0:T(1024)S(1)}, f32[640]{0:T(1024)}, u32[]{:S(2)}) copy-start(f32[640]{0:T(1024)} %param.42) | copy-start | bytes 7684
  119.2 7.8 %copy-start.5 = (bf16[16,3200]{1,0:T(8,128)(2,1)S(1)}, bf16[16,3200]{1,0:T(8,128)(2,1)}, u32[]{:S(2)}) copy-start(bf16[16,3200]{1,0:T(8,128)(2,1)} %param.27) | copy-start | bytes 307204
  122.2 65.1 %copy-start.8 = (f32[2560]{0:T(1024)S(1)}, f32[2560]{0:T(1024)}, u32[]{:S(2)}) copy-start(f32[2560]{0:T(1024)} %param.43) | copy-start | bytes 30724
  123.5 25.6 %all-to-all-start.1 = ((f32[8,16,2560]{2,1,0:T(8,128)}), f32[8,16,2560]{2,1,0:T(8,128)S(1)}, u32[]{:S(2)}, u32[]{:S(2)}) async-start(f32[8,16,2560]{2,1,0:T(8,128)} %broadcast_in_dim.16), calls=%async_computation.1 | async-start | bytes 2621440 | tf_op jit(solution)/shard_map/all_to_all | solution.py:21
  149.3 46.1 %copy-start.15 = (s32[16]{0:T(128)S(1)}, s32[16]{0:T(128)}, u32[]{:S(2)}) copy-start(s32[16]{0:T(128)} %param.26) | copy-start | bytes 196
  149.3 53.6 %slice-start = ((bf16[2560,2186]{1,0:T(8,128)(2,1)}), bf16[2560,10]{1,0:T(8,128)(2,1)S(1)}, s32[]{:S(2)}) async-start(bf16[2560,2186]{1,0:T(8,128)(2,1)} %all-gather.3.cloned.1.call-done), calls=%async_computation.5 | async-start | bytes 1310720 | tf_op jit(solution)/shard_map/slice | solution.py:14
  196.3 14.3 %all-to-all-start.2 = ((f32[8,6,16]{2,1,0:T(8,128)}), f32[8,6,16]{2,1,0:T(8,128)S(1)}, u32[]{:S(2)}, u32[]{:S(2)}) async-start(f32[8,6,16]{2,1,0:T(8,128)} %broadcast_in_dim.18), calls=%async_computation.2 | async-start | bytes 65536 | tf_op jit(solution)/shard_map/all_to_all | solution.py:21
Sparse Core Ops, SparseCore 0:
  10.3 70.6 all-gather.2
  82.7 104.5 all-gather.4
where the time goes:
time: 220 us; the launch traced here: 219 us
  waiting for transfers between devices  137 us (62%)
  local copies, waits for them, and re-layouts  19.7 us (9%)
  matrix products  16.4 us (7%)
  between operations  14.3 us (6%)
  blocking collectives  14.1 us (6%)
  starting transfers between devices  10.2 us (5%)
  other arithmetic  7.78 us (4%)
    all_gather x1, waiting for transfers between devices, sent_together(): result, at, done = (lax.all_gather(both, axis, axis=dim, tiled=True), 0, [])  69.3 us
    all_gather x1, waiting for transfers between devices, shards(): lax.all_gather(lm_head, 'group', axis=1, tiled=True)  38 us
    all_to_all x2, waiting for transfers between devices, from_everyone(): lax.all_to_all(jnp.broadcast_to(array[None], (peers, *array.shape)), axis...  28.6 us
    all_to_all x1, blocking collectives, from_everyone(): lax.all_to_all(jnp.broadcast_to(array[None], (peers, *array.shape)), axis...  14.1 us
    all_to_all x2, starting transfers between devices, from_everyone(): lax.all_to_all(jnp.broadcast_to(array[None], (peers, *array.shape)), axis...  10.2 us
    dot_general x1, matrix products, shards(): lax.dot_general(final_hidden, lax.all_gather(lm_head, 'group', axis=1, ti...  8.03 us
    slice x4, local copies, waits for them, and re-layouts, sent_together(): done.append(lax.slice_in_dim(result, at, at + a.shape[along], axis=along))  7.68 us
    unnamed x36, local copies, waits for them, and re-layouts  5.83 us
  transfers between devices with their start and end apart: 4, of which 4 were waited for; matrix products, arithmetic and copies ran while one was open for 12% of the time, Pallas kernels for 0%

commit v1 on v0

--- a/solution.py
+++ b/solution.py
@@ -141,7 +141,9 @@
     vocab_local = lm_head.shape[0]
     logits = lax.dot_general(
         final_hidden,
-        lax.all_gather(lm_head, "group", axis=1, tiled=True),
+        jnp.concatenate(
+            lax.all_to_all(jnp.stack([lm_head] * lax.axis_size("group")), "group", 0, 0), axis=1
+        ),
         (((1,), (1,)), ((), ())),
         preferred_element_type=jnp.float32,
     )

time: 220 us -> 450 us (2.05)
  waiting for transfers between devices: 137 us -> 339 us
  blocking collectives: 14.1 us -> 35.6 us
  local copies, waits for them, and re-layouts: 19.7 us -> 26.3 us
    all_to_all x0 -> x1, waiting for transfers between devices: none -> 264 us  [shards(): lax.all_to_all(jnp.stack([lm_head] * lax.axis_size('group')), 'group', 0, 0)]
    all_gather x1 -> x0, waiting for transfers between devices: 38 us -> none  [shards(): lax.all_gather(lm_head, 'group', axis=1, tiled=True)]
    all_to_all x2 -> x1, waiting for transfers between devices: 28.6 us -> 6.73 us  [from_everyone(): lax.all_to_all(jnp.broadcast_to(array[None], (peers, *array.shape)), axis...]
    all_to_all x1 -> x2, blocking collectives: 14.1 us -> 35.6 us  [from_everyone(): lax.all_to_all(jnp.broadcast_to(array[None], (peers, *array.shape)), axis...]
    all_to_all x2 -> x1, starting transfers between devices: 10.2 us -> 3.32 us  [from_everyone(): lax.all_to_all(jnp.broadcast_to(array[None], (peers, *array.shape)), axis...]
    another operation x0 -> x1, local copies, waits for them, and re-layouts: none -> 5.77 us  [shards(): jnp.stack([lm_head] * lax.axis_size('group'))]
    all_to_all x0 -> x1, starting transfers between devices: none -> 5.26 us  [shards(): lax.all_to_all(jnp.stack([lm_head] * lax.axis_size('group')), 'group', 0, 0)]
  transfers between devices with their start and end apart: 4 -> 3, of which waited for: 4 -> 3; matrix products, arithmetic and copies ran while one was open for 12% -> 1% of each run, Pallas kernels for 0% -> 0%
where the time goes in v1:
time: 450 us; the launch traced here: 449 us
  waiting for transfers between devices  339 us (75%)
  blocking collectives  35.6 us (8%)
  local copies, waits for them, and re-layouts  26.3 us (6%)
  matrix products  17.1 us (4%)
  between operations  14.3 us (3%)
  starting transfers between devices  8.62 us (2%)
  other arithmetic  7.96 us (2%)
    all_to_all x1, waiting for transfers between devices, shards(): lax.all_to_all(jnp.stack([lm_head] * lax.axis_size('group')), 'group', 0, 0)  264 us
    all_gather x1, waiting for transfers between devices, sent_together(): result, at, done = (lax.all_gather(both, axis, axis=dim, tiled=True), 0, [])  67.8 us
    all_to_all x2, blocking collectives, from_everyone(): lax.all_to_all(jnp.broadcast_to(array[None], (peers, *array.shape)), axis...  35.6 us
  transfers between devices with their start and end apart: 3, of which 3 were waited for; matrix products, arithmetic and copies ran while one was open for 1% of the time, Pallas kernels for 0%

profile of v1, /device:TPU:0, one launch (start us, length us, event | category | flops | bytes accessed | tf_op | source)
XLA Modules:
  0.0 448.6 jit_solution(14788566867504466074)
XLA Ops:
  7.2 0.8 copy.51
  8.1 2.1 concatenate.12
  10.2 1.2 exp.69
  11.3 0.8 add.148
  12.1 1.0 fusion.9
  13.1 67.8 %all-gather.2.cloned.1.call-done = bf16[2560,2186]{1,0:T(8,128)(2,1)} async-done(((bf16[160,2186]{1,0:T(8,128)(2,1)}), bf16[2560,2186]{1,0:T(8,128)(2,1)}) %all-gather.2.cloned.1.call-update) | async-done | bytes 11192336 | tf_op jit(solution)/shard_map/all_gather | solution.py:12
  81.0 1.4 slice.210
  82.4 1.3 fusion.2
  83.7 0.6 fusion.28
  84.4 6.3 %fusion.26 = (bf16[2560,640]{1,0:T(8,128)(2,1)S(1)}, bf16[2560,640]{1,0:T(8,128)(2,1)}, bf16[2560,640]{1,0:T(8,128)(2,1)S(1)}) fusion(bf16[2560,2186]{1,0:T(8,128)(2,1)} %all-gather.2.cloned.1.call-done), kind=kLoop, calls=%fused_computation.67 | loop fusion | bytes 19660800 | tf_op jit(solution)/shard_map/slice | solution.py:14
  90.7 1.7 copy-done.2
  92.4 0.6 fusion.1
  93.1 1.4 multiply_exponential_fusion
  94.6 4.2 multiply_add_fusion
  98.8 2.3 copy-done
  101.1 2.1 fusion.30
  103.3 0.7 bitcast_add_fusion
  104.0 1.0 reshape.151
  105.0 0.7 multiply_reduce_fusion.3
  105.7 14.3 %all_to_all.21 = f32[8,1,16]{2,1,0:T(1,128)S(1)} all-to-all(f32[8,1,16]{2,1,0:T(1,128)S(1)} %broadcast_in_dim.15), channel_id=1, replica_groups=mesh['group'=16,'head'=8] {'head'}, dimensions={0} | all-to-all | bytes 1024 | tf_op jit(solution)/shard_map/all_to_all | solution.py:21
  120.0 2.9 fusion.15
  123.1 21.3 %all_to_all.22 = f32[8,16,2560]{2,1,0:T(8,128)S(1)} all-to-all(f32[8,16,2560]{2,1,0:T(8,128)S(1)} %broadcast_in_dim.16), channel_id=1, replica_groups=mesh['group'=16,'head'=8] {'head'}, dimensions={0} | all-to-all | bytes 2621440 | tf_op jit(solution)/shard_map/all_to_all | solution.py:21
  144.4 5.8 %stack.2 = bf16[16,3200,160]{1,2,0:T(8,128)(2,1)} broadcast(bf16[3200,160]{0,1:T(8,128)(2,1)S(1)} %copy-done.5), dimensions={1,2} | broadcast | bytes 17408000 | tf_op jit(solution)/shard_map/stack | solution.py:145
  150.2 5.3 %all-to-all-start.2 = ((bf16[16,3200,160]{1,2,0:T(8,128)(2,1)}), bf16[16,3200,160]{1,2,0:T(8,128)(2,1)}, u32[]{:S(2)}, u32[]{:S(2)}) async-start(bf16[16,3200,160]{1,2,0:T(8,128)(2,1)} %stack.2), calls=%async_computation.2 | async-start | bytes 32768000 | tf_op jit(solution)/shard_map/all_to_all | solution.py:145
  155.9 264.1 %all-to-all-done.2 = bf16[16,3200,160]{1,2,0:T(8,128)(2,1)} async-done(((bf16[16,3200,160]{1,2,0:T(8,128)(2,1)}), bf16[16,3200,160]{1,2,0:T(8,128)(2,1)}, u32[]{:S(2)}, u32[]{:S(2)}) %all-to-all-start.2) | async-done | bytes 16384032 | tf_op jit(solution)/shard_map/all_to_all | solution.py:145
  420.0 8.1 %fusion.29 = (f32[16]{0:T(128)S(1)}, f32[16,3200]{1,0:T(8,128)S(1)}) fusion(bf16[3200,2560]{0,1:T(8,128)(2,1)} %bitcast.7, f32[16,2560]{1,0:T(8,128)S(1)} %reduce_sum.107, bf16[16,2560]{1,0:T(8,128)(2,1)S(1)} %copy-done.4, f32[2560]{0:T(1024)S(1)} %copy-done.9, f32[16]{0:T(128)S(1)} %add_rsqrt_fusion), kind=kOutput, calls=%fused_computation.70 | convolution fusion | flops 262399984 | bytes 16844928 | tf_op jit(solution)/shard_map/dot_general | solution.py:142
  428.4 0.6 broadcast_in_dim.18
  429.1 3.3 all-to-all-start.3
  432.4 0.9 copy.59
  433.3 6.7 %all-to-all-done.3 = f32[8,6,16]{2,1,0:T(8,128)S(1)} async-done(((f32[8,6,16]{2,1,0:T(8,128)}), f32[8,6,16]{2,1,0:T(8,128)S(1)}, u32[]{:S(2)}, u32[]{:S(2)}) %all-to-all-start.3) | async-done | bytes 3104 | tf_op jit(solution)/shard_map/all_to_all | solution.py:21
  440.7 0.5 subtract_bitcast_fusion
  441.3 0.5 add_bitcast_fusion
  (89 shorter events, 1.9 us)
Async XLA Ops:
  7.2 76.5 %copy-start.14 = (f32[4,256]{1,0:T(4,128)S(1)}, f32[4,256]{1,0:T(4,128)}, u32[]{:S(2)}) copy-start(f32[4,256]{1,0:T(4,128)} %param.36) | copy-start | bytes 12292
  7.2 76.5 %copy-start.11 = (bf16[16,3,256]{2,0,1:T(8,128)(2,1)S(1)}, bf16[16,3,256]{2,0,1:T(8,128)(2,1)}, u32[]{:S(2)}) copy-start(bf16[16,3,256]{2,0,1:T(8,128)(2,1)} %param.25) | copy-start | bytes 73732
  7.2 76.5 %copy-start.15 = (f32[256]{0:T(256)S(1)}, f32[256]{0:T(256)}, u32[]{:S(2)}) copy-start(f32[256]{0:T(256)} %param.37) | copy-start | bytes 3076
  7.2 73.8 %all-gather.2.cloned.1.call-start = ((), (), s32[]{:S(2)}) async-start(), calls=%async_computation.4 | async-start | bytes 12533760 | tf_op jit(solution)/shard_map/all_gather | solution.py:12
  82.4 1.4 copy-start.3
  84.4 8.0 %copy-start.4 = (bf16[16,2560]{1,0:T(8,128)(2,1)S(1)}, bf16[16,2560]{1,0:T(8,128)(2,1)}, u32[]{:S(2)}) copy-start(bf16[16,2560]{1,0:T(8,128)(2,1)} %param.22) | copy-start | bytes 245764
  84.4 8.0 %copy-start.7 = (f32[2560]{0:T(1024)S(1)}, f32[2560]{0:T(1024)}, u32[]{:S(2)}) copy-start(f32[2560]{0:T(1024)} %param.41) | copy-start | bytes 30724
  84.4 8.6 %copy-start.8 = (bf16[16,3,640]{2,0,1:T(8,128)(2,1)S(1)}, bf16[16,3,640]{2,0,1:T(8,128)(2,1)}, u32[]{:S(2)}) copy-start(bf16[16,3,640]{2,0,1:T(8,128)(2,1)} %param.24) | copy-start | bytes 184324
  84.4 8.6 %copy-start.12 = (f32[4,640]{1,0:T(4,128)S(1)}, f32[4,640]{1,0:T(4,128)}, u32[]{:S(2)}) copy-start(f32[4,640]{1,0:T(4,128)} %param.34) | copy-start | bytes 30724
  90.7 1.7 copy-start.2
  90.7 14.3 %copy-start.1 = (bf16[2560,640]{1,0:T(8,128)(2,1)}, bf16[2560,640]{1,0:T(8,128)(2,1)S(1)}, u32[]{:S(2)}) copy-start(bf16[2560,640]{1,0:T(8,128)(2,1)S(1)} %get-tuple-element.62) | copy-start | bytes 9830404
  94.6 6.6 %copy-start.10 = (f32[16,128]{1,0:T(8,128)S(1)}, f32[16,128]{1,0:T(8,128)}, u32[]{:S(2)}) copy-start(f32[16,128]{1,0:T(8,128)} %get-tuple-element.71) | copy-start | bytes 24580
  98.8 2.4 copy-start
  98.8 4.5 copy-start.16
  98.8 21.2 %copy-start.13 = (f32[640]{0:T(1024)S(1)}, f32[640]{0:T(1024)}, u32[]{:S(2)}) copy-start(f32[640]{0:T(1024)} %param.42) | copy-start | bytes 7684
  105.7 38.7 %copy-start.5 = (bf16[3200,160]{0,1:T(8,128)(2,1)S(1)}, bf16[3200,160]{0,1:T(8,128)(2,1)}, u32[]{:S(2)}) copy-start(bf16[3200,160]{0,1:T(8,128)(2,1)} %param.33) | copy-start | bytes 3072004
  150.2 5.3 %copy-start.6 = (bf16[16,3200]{1,0:T(8,128)(2,1)S(1)}, bf16[16,3200]{1,0:T(8,128)(2,1)}, u32[]{:S(2)}) copy-start(bf16[16,3200]{1,0:T(8,128)(2,1)} %param.27) | copy-start | bytes 307204
  150.2 269.8 %copy-start.9 = (f32[2560]{0:T(1024)S(1)}, f32[2560]{0:T(1024)}, u32[]{:S(2)}) copy-start(f32[2560]{0:T(1024)} %param.43) | copy-start | bytes 30724
  150.2 269.8 %all-to-all-start.2 = ((bf16[16,3200,160]{1,2,0:T(8,128)(2,1)}), bf16[16,3200,160]{1,2,0:T(8,128)(2,1)}, u32[]{:S(2)}, u32[]{:S(2)}) async-start(bf16[16,3200,160]{1,2,0:T(8,128)(2,1)} %stack.2), calls=%async_computation.2 | async-start | bytes 32768000 | tf_op jit(solution)/shard_map/all_to_all | solution.py:145
  420.0 8.1 %copy-start.17 = (s32[16]{0:T(128)S(1)}, s32[16]{0:T(128)}, u32[]{:S(2)}) copy-start(s32[16]{0:T(128)} %param.26) | copy-start | bytes 196
  420.0 12.4 %slice-start = ((bf16[2560,2186]{1,0:T(8,128)(2,1)}), bf16[2560,10]{1,0:T(8,128)(2,1)S(1)}, s32[]{:S(2)}) async-start(bf16[2560,2186]{1,0:T(8,128)(2,1)} %all-gather.2.cloned.1.call-done), calls=%async_computation.5 | async-start | bytes 1310720 | tf_op jit(solution)/shard_map/slice | solution.py:14
  429.1 11.0 %all-to-all-start.3 = ((f32[8,6,16]{2,1,0:T(8,128)}), f32[8,6,16]{2,1,0:T(8,128)S(1)}, u32[]{:S(2)}, u32[]{:S(2)}) async-start(f32[8,6,16]{2,1,0:T(8,128)} %broadcast_in_dim.18), calls=%async_computation.3 | async-start | bytes 65536 | tf_op jit(solution)/shard_map/all_to_all | solution.py:21
Sparse Core Ops, SparseCore 0:
  10.3 70.6 all-gather.1
